TPU v7x, 128 devices: a whole 4x4x4 slice. The times are simulated.
128 devices in a mesh: row: 8 (over y, core), col: 16 (over z, x).
Axes of the slice: x: 4, y: 4, z: 4, core: 2. Of those that a mesh axis runs over, the one named last changes fastest.
Arguments:
- images: bfloat16 [16384, 768], P(('row', 'col')), may hold values from -5 to 5
- texts: bfloat16 [16384, 768], P(('col', 'row')), may hold values from -5 to 5
- audio: bfloat16 [16384, 768], P(('col', 'row')), may hold values from -5 to 5
Outputs:
- grad_images: float32 [16384, 768], P(('row', 'col'))
- grad_texts: float32 [16384, 768], P(('col', 'row'))
- grad_audio: float32 [16384, 768], P(('col', 'row'))
All inputs are finite; a program needn't handle non-finite values.
Results may differ from a plain program's by a relative error of at most 0.013.
Values may be sent and summed in bfloat16 or wider, within the bound.
A program may use at most 128 MiB of HBM per device.

v0:
```python
import functools

import jax
import jax.numpy as jnp
from jax import lax
from jax.experimental import pallas as pl
from jax.experimental.pallas import tpu as pltpu
from jax.sharding import PartitionSpec as P

ITERS = 3
logit_softness = 0.07
target_softness = 0.05
epsilon = 1e-06
LOG2E = 1.4426950408889634

MESH = pl.DeviceIdType.MESH
F32 = jnp.float32
BF16 = jnp.bfloat16
B = 128
D = 768
POS = [(2, 2), (1, 2), (3, 2), (0, 2), (2, 1), (2, 3), (2, 0), (1, 1), (1, 3), (3, 1), (3, 3), (0, 1), (0, 3), (1, 0), (3, 0), (0, 0)]
PI = {p: i for i, p in enumerate(POS)}
COLS = [(2, 0), (2, 1), (1, 0), (1, 1), (3, 0), (3, 1), (0, 0), (0, 1)]
CI = {p: i for i, p in enumerate(COLS)}
NSEM = 144
UNROLL = 4


class Net:
    def __init__(self, send_sem, recv_sem):
        self.send_sem, self.recv_sem = send_sem, recv_sem
        self.index, self.sent = {}, []

    def at(self, tag):
        return self.index.setdefault(tag, len(self.index))

    def copy(self, tag, src, dst, device):
        i = self.at(tag)
        return pltpu.make_async_remote_copy(
            src_ref=src, dst_ref=dst, send_sem=self.send_sem.at[i], recv_sem=self.recv_sem.at[i],
            device_id=device, device_id_type=MESH,
        )

    def send(self, tag, src, dst, device):
        self.sent.append((tag, src, dst, device))
        self.make(tag, src, dst, device).start()

    def make(self, tag, src, dst, device):
        return self.copy(tag, src() if callable(src) else src, dst() if callable(dst) else dst, device)

    def wait(self, tag, landed, device):
        self.copy(tag, landed, landed, device).wait_recv()

    def drain(self):
        for entry in self.sent:
            self.make(*entry).wait_send()


def unit_of(raw_ref):
    values = raw_ref[...].astype(F32)
    inverse = lax.rsqrt(jnp.sum(values * values, axis=1, keepdims=True) + epsilon)
    return values * inverse, inverse


def lanes_to_rows(row):
    return jnp.broadcast_to(row, (B, B)).T


def kernel(
    img_hbm, txt_hbm, aud_hbm, img_out, txt_out, aud_out,
    img_in, txt_in, aud_in, out_img, out_txt, out_aud, in_sem, out_sem,
    img, cols, K, E, S,
    rows_local, rows_turned, rows_sent, rows_got, cols_local, cols_sent, cols_got, avec, avec_turned, bvec, rho, ict, U,
    st1, r1, st2, r2, st3, r3, st4, r4,
    gsib, sibgot, yst1, yr1, yst2, yr2,
    net_send, net_recv, rsend, rrecv, csend, crecv,
):
    row, col = lax.axis_index("row"), lax.axis_index("col")
    y, core = row // 2, lax.rem(row, 2)
    z, x = col // 4, lax.rem(col, 4)

    def wrap(v):
        return lax.rem(v, 4)

    def zx(dz, dx):
        return wrap(z + dz) * 4 + wrap(x + dx)

    def yc(dy, own):
        return wrap(y + dy) * 2 + (core if own else 1 - core)

    col_of = [zx(dz, dx) for dz, dx in POS]
    row_of = [yc(dy, own) for dy, own in COLS]

    def at_zx(dz, dx):
        return (row, col_of[PI[dz % 4, dx % 4]])

    def at_y(dy, own=1):
        return (row_of[CI[dy % 4, own]], col)

    loads = [
        pltpu.make_async_copy(src, dst, in_sem.at[i])
        for i, (src, dst) in enumerate(((img_hbm, img_in), (txt_hbm, txt_in), (aud_hbm, aud_in)))
    ]
    for load in loads:
        load.start()

    barrier = pltpu.get_barrier_semaphore()
    near = [at_zx(1, 0), at_zx(3, 0), at_zx(0, 1), at_zx(0, 3), at_y(1), at_y(3), at_y(0, 0)]
    for device in near:
        pl.semaphore_signal(barrier, inc=1, device_id=device, device_id_type=MESH)

    def image(dz, dx, start=0, count=B):
        return img.at[pl.ds(PI[dz % 4, dx % 4] * B + start, count), :]

    def column(m, dy, own, start=0, count=B):
        return cols.at[pl.ds(m * 1024 + CI[dy % 4, own] * B + start, count), :]

    loads[0].wait()
    image(0, 0)[...] = unit_of(img_in)[0].astype(BF16)
    loads[1].wait()
    column(0, 0, 1)[...] = unit_of(txt_in)[0].astype(BF16)
    loads[2].wait()
    column(1, 0, 1)[...] = unit_of(aud_in)[0].astype(BF16)
    pl.semaphore_wait(barrier, len(near))

    net = Net(net_send, net_recv)

    def place(h, first, second):
        return (first, second) if h == 0 else (second, first)

    def half_dev(h, first, second):
        return at_zx(*place(h, first, second))

    def first_send(h):
        for step in (1, 3):
            net.send(("g1", h, step), image(0, 0, 64 * h, 64), image(*place(h, -step, 0), 64 * h, 64), half_dev(h, step, 0))

    def second_send(h, f):
        for step in (1, 3):
            net.send(("g2", h, f, step), image(*place(h, f, 0), 64 * h, 64), image(*place(h, f, -step), 64 * h, 64), half_dev(h, 0, step))

    def first_forward(h, step):
        net.wait(("g1", h, step), image(*place(h, -step, 0), 64 * h, 64), half_dev(h, -step, 0))
        at = 64 * h + (0 if step == 1 else 32)
        net.send(("g1f", h, step), image(*place(h, -step, 0), at, 32), image(*place(h, 2, 0), at, 32), half_dev(h, step, 0))

    def first_end(h):
        for step in (1, 3):
            at = 64 * h + (0 if step == 1 else 32)
            net.wait(("g1f", h, step), image(*place(h, 2, 0), at, 32), half_dev(h, -step, 0))

    def second_forward(h, f):
        for step in (1, 3):
            net.wait(("g2", h, f, step), image(*place(h, f, -step), 64 * h, 64), half_dev(h, 0, -step))
            at = 64 * h + (0 if step == 1 else 32)
            net.send(("g2f", h, f, step), image(*place(h, f, -step), at, 32), image(*place(h, f, 2), at, 32), half_dev(h, 0, step))

    def second_end(h, f):
        for step in (1, 3):
            at = 64 * h + (0 if step == 1 else 32)
            net.wait(("g2f", h, f, step), image(*place(h, f, 2), at, 32), half_dev(h, 0, -step))

    def col_send(m):
        for step in (1, 3):
            net.send(("c1", m, step), column(m, 0, 1), column(m, -step, 1), at_y(step))
        net.send(("cs", m, 0), column(m, 0, 1), column(m, 0, 0), at_y(0, 0))

    def col_forward(m):
        for step in (1, 3):
            net.wait(("c1", m, step), column(m, -step, 1), at_y(-step))
            at = 0 if step == 1 else 64
            net.send(("c1f", m, step), column(m, -step, 1, at, 64), column(m, 2, 1, at, 64), at_y(step))
            net.send(("cs", m, -step % 4), column(m, -step, 1), column(m, -step, 0), at_y(0, 0))

    def col_end(m):
        for step in (1, 3):
            at = 0 if step == 1 else 64
            net.wait(("c1f", m, step), column(m, 2, 1, at, 64), at_y(-step))
        net.send(("cs", m, 2), column(m, 2, 1), column(m, 2, 0), at_y(0, 0))

    def col_near(m):
        for dy in (0, 1, 3):
            net.wait(("cs", m, dy), column(m, dy, 0), at_y(0, 0))

    def col_far(m):
        net.wait(("cs", m, 2), column(m, 2, 0), at_y(0, 0))

    def tile(j):
        return slice(j * B, (j + 1) * B)

    def row_part(part):
        return jnp.sum(part.T, axis=0, keepdims=True)

    def block(i):
        return pl.ds(pl.multiple_of(i * B, B), B)

    contract = (((1,), (1,)), ((), ()))

    def similarity(m, lo, hi, left, right, first):
        def body(i, carry):
            at = pl.ds(pl.multiple_of(i * 256, 256), 256)
            cosine = lax.dot_general(
                img[at, :], cols[m * 1024 + left : m * 1024 + right, :], contract, preferred_element_type=F32
            )
            part = jnp.zeros((256, B), F32)
            for j in range((right - left) // B):
                piece = cosine[:, tile(j)]
                kern = jnp.exp2(piece * (LOG2E / target_softness))
                K[m, at, left + j * B : left + (j + 1) * B] = kern
                soft = jnp.exp2(piece * (LOG2E / logit_softness))
                E[at, m * 1024 + left + j * B : m * 1024 + left + (j + 1) * B] = soft.astype(BF16)
                part = part + kern
            for t in (0, 1):
                total = row_part(part[t * B : (t + 1) * B])
                if not first:
                    total = total + rows_local[m, pl.ds(2 * i + t, 1), :]
                rows_local[m, pl.ds(2 * i + t, 1), :] = total
            return carry

        lax.fori_loop(lo, hi, body, 0)

    for h in (0, 1):
        first_send(h)
    col_send(0)
    for h in (0, 1):
        second_send(h, 0)
    col_send(1)
    for step in (1, 3):
        for h in (0, 1):
            first_forward(h, step)
    for f in (3, 1):
        for h in (0, 1):
            second_send(h, f)
    col_forward(0)
    for h in (0, 1):
        second_forward(h, 0)
    for h in (0, 1):
        first_end(h)
        second_send(h, 2)
    col_near(0)
    similarity(0, 6, 8, 256, 1024, True)
    for h in (0, 1):
        second_forward(h, 3)
    col_forward(1)
    for h in (0, 1):
        second_forward(h, 1)
    col_near(1)
    similarity(1, 6, 8, 256, 1024, True)
    col_end(0)
    similarity(0, 4, 6, 256, 1024, True)
    for h in (0, 1):
        second_forward(h, 2)
    col_end(1)
    similarity(1, 4, 6, 256, 1024, True)
    for h in (0, 1):
        second_end(h, 0)
    for m in (0, 1):
        similarity(m, 3, 4, 256, 1024, True)
    for m in (0, 1):
        col_far(m)
        similarity(m, 3, 8, 0, 256, False)
    for f in (3, 1):
        for h in (0, 1):
            second_end(h, f)
    for m in (0, 1):
        similarity(m, 1, 3, 0, 1024, True)
    for h in (0, 1):
        second_end(h, 2)

    def rows_send(k, m):
        for i in range(16):
            rows_turned[m, pl.ds(col_of[i], 1), :] = rows_local[m, i : i + 1, :]
        rows_sent[k, m] = rows_turned[m].astype(BF16)
        for i in range(15):
            pltpu.make_async_remote_copy(
                src_ref=rows_sent.at[k, m], dst_ref=rows_got.at[k, m, i], send_sem=rsend.at[k, m], recv_sem=rrecv.at[k, m],
                device_id=(row, col_of[i]), device_id_type=MESH,
            ).start()

    def rows_whole(k, m):
        return pltpu.make_async_remote_copy(
            src_ref=rows_got.at[k, m], dst_ref=rows_got.at[k, m], send_sem=rsend.at[k, m], recv_sem=rrecv.at[k, m],
            device_id=(row, col_of[0]), device_id_type=MESH,
        )

    def rows_sum(k, m):
        rows_whole(k, m).wait_recv()
        return rows_sent[k, m].astype(F32) + jnp.sum(rows_got[k, m].astype(F32), axis=0)

    def cols_send(k, m):
        for i in range(8):
            cols_sent[k, m, pl.ds(row_of[i], 1), :] = cols_local[m, i : i + 1, :]
        for i in range(7):
            pltpu.make_async_remote_copy(
                src_ref=cols_sent.at[k, m], dst_ref=cols_got.at[k, m, i], send_sem=csend.at[k, m], recv_sem=crecv.at[k, m],
                device_id=(row_of[i], col), device_id_type=MESH,
            ).start()

    def cols_whole(k, m):
        return pltpu.make_async_remote_copy(
            src_ref=cols_got.at[k, m], dst_ref=cols_got.at[k, m], send_sem=csend.at[k, m], recv_sem=crecv.at[k, m],
            device_id=(row_of[0], col), device_id_type=MESH,
        )

    def cols_sum(k, m):
        cols_whole(k, m).wait_recv()
        return cols_sent[k, m] + jnp.sum(cols_got[k, m], axis=0)

    def rows_back(dst, m, value):
        rows_local[m] = value
        for i in range(16):
            dst[m, i : i + 1, :] = rows_local[m, pl.ds(col_of[i], 1), :]

    def cols_back(dst, m, value):
        cols_local[m] = value
        for i in range(8):
            dst[m, i : i + 1, :] = cols_local[m, pl.ds(row_of[i], 1), :]

    def fold(value):
        return jnp.sum(value.reshape(16, 8, B), axis=0)

    def close_columns(m, acc):
        for j in range(8):
            cols_local[m, j : j + 1, :] = jnp.sum(acc[j], axis=0, keepdims=True)

    def side(m, j):
        return slice(m * 1024 + j * B, m * 1024 + (j + 1) * B)

    zeros = tuple(jnp.zeros((8, B), F32) for _ in range(8))

    def over_blocks(one, carry):
        def body(t, carry):
            for u in range(UNROLL):
                carry = one(t * UNROLL + u, carry)
            return carry

        return lax.fori_loop(0, 16 // UNROLL, body, carry)

    def softmax(m):
        def one(i, acc):
            part = jnp.zeros((B, B), F32)
            out = []
            for j in range(8):
                e = E[block(i), side(m, j)].astype(F32)
                part = part + e
                out.append(acc[j] + fold(e))
            rows_local[m, pl.ds(i, 1), :] = row_part(part)
            return tuple(out)

        close_columns(m, over_blocks(one, zeros))

    def column_pass(m):
        def one(i, acc):
            a = lanes_to_rows(avec[m, pl.ds(i, 1), :])
            return tuple(acc[j] + fold(K[m, block(i), tile(j)] * a) for j in range(8))

        close_columns(m, over_blocks(one, zeros))

    def row_pass(m):
        def one(i, carry):
            part = K[m, block(i), tile(0)] * bvec[m, 0:1, :]
            for j in range(1, 8):
                part = part + K[m, block(i), tile(j)] * bvec[m, j : j + 1, :]
            rows_local[m, pl.ds(i, 1), :] = row_part(part)
            return carry

        over_blocks(one, 0)

    def soft_steps(lo, hi):
        def body(t, carry):
            m, i = t // 8, lax.rem(t, 8)
            at = pl.ds(pl.multiple_of(i * 256, 256), 256)
            here = pl.ds(pl.multiple_of(m * 1024, 1024), 1024)
            U[m, at, :] = jnp.dot(E[at, here], cols[here, :], preferred_element_type=F32).astype(BF16)
            return carry

        lax.fori_loop(lo, hi, body, 0)

    both = (0, 1)
    for m in both:
        similarity(m, 0, 1, 0, 1024, True)
        rows_send(0, m)
    for m in both:
        softmax(m)
        rows_send(ITERS + 1, m)
        cols_send(ITERS, m)
    cuts = [0, 3, 6, 9, 12, 16]
    for sweep in range(ITERS):
        for m in both:
            avec_turned[m] = 1.0 / rows_sum(sweep, m)
            rows_back(avec, m, avec_turned[m])
            column_pass(m)
            cols_send(sweep, m)
        soft_steps(cuts[2 * sweep], cuts[2 * sweep + 1])
        for m in both:
            cols_back(bvec, m, 1.0 / cols_sum(sweep, m))
            row_pass(m)
            rows_send(sweep + 1, m)
        if sweep < ITERS - 1:
            soft_steps(cuts[2 * sweep + 1], cuts[2 * sweep + 2])
    for m in both:
        cols_back(ict, m, 1.0 / cols_sum(ITERS, m))

    def score(i):
        for b in (2 * i, 2 * i + 1):
            at = slice(b * B, (b + 1) * B)
            for m in both:
                a = lanes_to_rows(avec[m, b : b + 1, :])
                twice = a + a
                for j in range(8):
                    soft = E[at, side(m, j)].astype(F32) * ict[m, j : j + 1, :]
                    target = K[m, at, tile(j)] * twice * bvec[m, j : j + 1, :]
                    S[at, side(m, j)] = (soft - target).astype(BF16)

    def whole_score(i):
        for b in (2 * i, 2 * i + 1):
            at = slice(b * B, (b + 1) * B)
            for m in both:
                mass = lanes_to_rows(rho[m, b : b + 1, :])
                for j in range(8):
                    soft = E[at, side(m, j)].astype(F32) * mass
                    E[at, side(m, j)] = (S[at, side(m, j)].astype(F32) + soft).astype(BF16)

    def part_of(h, first, second, start=0, count=64):
        dz, dx = place(h, first % 4, second % 4)
        at = PI[dz, dx] * B + 64 * h + start
        return K[0, at : at + count, 0:D]

    def near_dev(h, step):
        return half_dev(h, 0, step)

    def far_dev(h, step):
        return half_dev(h, step, 0)

    def reduce1(h, f):
        st1[h, f] = part_of(h, f, 2).astype(BF16)
        for s, step in enumerate((1, 3)):
            net.send(
                ("r1", h, f, s), lambda s=s: st1.at[h, f, pl.ds(32 * s, 32), :], lambda s=s: r1.at[h, f, s], near_dev(h, step)
            )

    def reduce2(h, f, s):
        step = (1, 3)[s]
        net.wait(("r1", h, f, s), r1.at[h, f, s], near_dev(h, -step))
        for t in (0, 1):
            value = part_of(h, f, step, 32 * t, 32)
            if s == t:
                value = value + r1[h, f, s].astype(F32)
            st2[h, f, s, 32 * t : 32 * t + 32, :] = value.astype(BF16)
        net.send(("r2", h, f, s), lambda: st2.at[h, f, s], lambda: r2.at[h, f, s], near_dev(h, step))

    def line(h, f):
        for s, step in enumerate((1, 3)):
            net.wait(("r2", h, f, s), r2.at[h, f, s], near_dev(h, -step))
        return part_of(h, f, 0) + r2[h, f, 0].astype(F32) + r2[h, f, 1].astype(F32)

    def reduce3(h):
        st3[h] = line(h, 2).astype(BF16)
        for s, step in enumerate((1, 3)):
            net.send(("r3", h, s), st3.at[h, pl.ds(32 * s, 32), :], r3.at[h, s], far_dev(h, step))

    def reduce4(h, s):
        step = (1, 3)[s]
        value = line(h, step)
        net.wait(("r3", h, s), r3.at[h, s], far_dev(h, -step))
        for t in (0, 1):
            piece = value[32 * t : 32 * t + 32]
            if s == t:
                piece = piece + r3[h, s].astype(F32)
            st4[h, s, 32 * t : 32 * t + 32, :] = piece.astype(BF16)
        net.send(("r4", h, s), st4.at[h, s], r4.at[h, s], far_dev(h, step))

    def reduce5(h):
        value = line(h, 0)
        for s, step in enumerate((1, 3)):
            net.wait(("r4", h, s), r4.at[h, s], far_dev(h, -step))
        return value + r4[h, 0].astype(F32) + r4[h, 1].astype(F32)

    def image_step(i, others):
        at = slice(i * 256, (i + 1) * 256)
        for n in range(3):
            out = slice(n * 256, (n + 1) * 256)
            total = jnp.dot(S[at, :], cols[:, out], preferred_element_type=F32)
            if n < len(others):
                others[n]()
            K[0, at, out] = total

    def add_soft(i):
        for b in (2 * i, 2 * i + 1):
            at = slice(b * B, (b + 1) * B)
            mass = [lanes_to_rows(rho[m, b : b + 1, :]) for m in both]
            for j in range(6):
                K[0, at, tile(j)] = (
                    K[0, at, tile(j)] + U[0, at, tile(j)].astype(F32) * mass[0] + U[1, at, tile(j)].astype(F32) * mass[1]
                )

    ORDER = (2, 1, 3, 0)

    def side_copy(m, k):
        return net.copy(("sib", m, k), gsib.at[m, k], sibgot.at[m, k], at_y(0, 0))

    def pair_sum(m, k):
        side_copy(m, k).wait_recv()
        at = (m * 4 + k) * B
        return K[1, at : at + B, 0:D] + sibgot[m, k].astype(F32)

    def ring1(m):
        yst1[m] = pair_sum(m, 0).astype(BF16)
        for s, step in enumerate((1, 3)):
            net.send(("y1", m, s), yst1.at[m, pl.ds(64 * s, 64), :], yr1.at[m, s], at_y(step))

    def ring2(m, s):
        step = (1, 3)[s]
        value = pair_sum(m, 1 + s)
        net.wait(("y1", m, s), yr1.at[m, s], at_y(-step))
        for t in (0, 1):
            piece = value[64 * t : 64 * t + 64]
            if s == t:
                piece = piece + yr1[m, s].astype(F32)
            yst2[m, s, 64 * t : 64 * t + 64, :] = piece.astype(BF16)
        net.send(("y2", m, s), yst2.at[m, s], yr2.at[m, s], at_y(step))

    def ring3(m):
        value = pair_sum(m, 3)
        for s, step in enumerate((1, 3)):
            net.wait(("y2", m, s), yr2.at[m, s], at_y(-step))
        return value + yr2[m, 0].astype(F32) + yr2[m, 1].astype(F32)

    down = (((0,), (0,)), ((), ()))

    def column_step(m, k):
        total = lax.dot_general(
            E[:, m * 1024 + k * 256 : m * 1024 + k * 256 + 256], img[...], down, preferred_element_type=F32
        )
        gsib[m, k] = total[:B].astype(BF16)
        K[1, (m * 4 + k) * B : (m * 4 + k + 1) * B, 0:D] = total[B:]
        net.send(("sib", m, k), gsib.at[m, k], sibgot.at[m, k], at_y(0, 0))

    def scores(*steps):
        return [functools.partial(score, i) for i in steps]

    def whole_scores(*steps):
        return [functools.partial(whole_score, i) for i in steps]

    score(0)
    image_step(0, scores(1, 2))
    image_step(1, scores(3, 4))
    image_step(2, scores(5, 6))
    image_step(3, scores(7))
    for m in both:
        rows_back(rho, m, avec_turned[m] * rows_sum(ITERS, m) / rows_sum(ITERS + 1, m))
    add_soft(0)
    reduce1(0, 2)
    reduce1(1, 2)
    reduce1(0, 1)
    add_soft(1)
    reduce1(0, 3)
    reduce1(0, 0)
    add_soft(2)
    reduce1(1, 1)
    reduce1(1, 3)
    add_soft(3)
    reduce1(1, 0)
    image_step(4, whole_scores(0, 1, 2))
    image_step(5, whole_scores(3, 4, 5))
    whole_score(6)
    whole_score(7)
    column_step(0, 0)
    add_soft(4)
    add_soft(5)
    for s in (0, 1):
        reduce2(0, 2, s)
        reduce2(1, 2, s)
    column_step(1, 0)
    ring1(0)
    for s in (0, 1):
        reduce2(0, 1, s)
        reduce2(1, 1, s)
    image_step(6, ())
    ring1(1)
    add_soft(6)
    for s in (0, 1):
        reduce2(0, 3, s)
        reduce2(1, 3, s)
    image_step(7, ())
    add_soft(7)
    for s in (0, 1):
        reduce2(0, 0, s)
        reduce2(1, 0, s)
    column_step(0, 1)
    column_step(0, 2)
    ring2(0, 0)
    reduce3(0)
    reduce3(1)
    column_step(1, 1)
    ring2(0, 1)
    column_step(1, 2)
    ring2(1, 0)
    for h in (0, 1):
        reduce4(h, 0)
    column_step(0, 3)
    ring2(1, 1)
    for h in (0, 1):
        reduce4(h, 1)
    column_step(1, 3)

    def finish(raw_ref, out_ref, rows, g):
        values = raw_ref[rows, :].astype(F32)
        inverse = lax.rsqrt(jnp.sum(values * values, axis=1, keepdims=True) + epsilon)
        unit = values * inverse
        g = g * (1.0 / logit_softness)
        out_ref[rows, :] = (g - unit * jnp.sum(unit * g, axis=1, keepdims=True)) * inverse

    stores = []

    def leave(src, dst):
        stores.append(pltpu.make_async_copy(src, dst, out_sem.at[len(stores)]))
        stores[-1].start()

    for h in (0, 1):
        finish(img_in, out_img, slice(64 * h, 64 * h + 64), reduce5(h))
    leave(out_img, img_out)
    finish(txt_in, out_txt, slice(0, B), ring3(0))
    leave(out_txt, txt_out)
    finish(aud_in, out_aud, slice(0, B), ring3(1))
    leave(out_aud, aud_out)

    net.drain()
    for m in both:
        for k in range(ITERS + 2):
            rows_whole(k, m).wait_send()
        for k in range(ITERS + 1):
            cols_whole(k, m).wait_send()
    for store in stores:
        store.wait()


def gradients(images, texts, audio):
    whole = pl.BlockSpec(memory_space=pl.ANY)
    shape = jax.ShapeDtypeStruct(images.shape, F32)
    rounds_r, rounds_c = ITERS + 2, ITERS + 1
    return pl.pallas_call(
        kernel,
        out_shape=(shape, shape, shape),
        in_specs=[whole] * 3,
        out_specs=[whole] * 3,
        scratch_shapes=[
            pltpu.VMEM((B, D), BF16),
            pltpu.VMEM((B, D), BF16),
            pltpu.VMEM((B, D), BF16),
            pltpu.VMEM((B, D), F32),
            pltpu.VMEM((B, D), F32),
            pltpu.VMEM((B, D), F32),
            pltpu.SemaphoreType.DMA((3,)),
            pltpu.SemaphoreType.DMA((3,)),
            pltpu.VMEM((2048, D), BF16),
            pltpu.VMEM((2048, D), BF16),
            pltpu.VMEM((2, 2048, 1024), F32),
            pltpu.VMEM((2048, 2048), BF16),
            pltpu.VMEM((2048, 2048), BF16),
            pltpu.VMEM((2, 16, B), F32),
            pltpu.VMEM((2, 16, B), F32),
            pltpu.VMEM((rounds_r, 2, 16, B), BF16),
            pltpu.VMEM((rounds_r, 2, 15, 16, B), BF16),
            pltpu.VMEM((2, 8, B), F32),
            pltpu.VMEM((rounds_c, 2, 8, B), F32),
            pltpu.VMEM((rounds_c, 2, 7, 8, B), F32),
            pltpu.VMEM((2, 16, B), F32),
            pltpu.VMEM((2, 16, B), F32),
            pltpu.VMEM((2, 8, B), F32),
            pltpu.VMEM((2, 16, B), F32),
            pltpu.VMEM((2, 8, B), F32),
            pltpu.VMEM((2, 2048, D), BF16),
            pltpu.VMEM((2, 4, 64, D), BF16),
            pltpu.VMEM((2, 4, 2, 32, D), BF16),
            pltpu.VMEM((2, 4, 2, 64, D), BF16),
            pltpu.VMEM((2, 4, 2, 64, D), BF16),
            pltpu.VMEM((2, 64, D), BF16),
            pltpu.VMEM((2, 2, 32, D), BF16),
            pltpu.VMEM((2, 2, 64, D), BF16),
            pltpu.VMEM((2, 2, 64, D), BF16),
            pltpu.VMEM((2, 4, B, D), BF16),
            pltpu.VMEM((2, 4, B, D), BF16),
            pltpu.VMEM((2, B, D), BF16),
            pltpu.VMEM((2, 2, 64, D), BF16),
            pltpu.VMEM((2, 2, B, D), BF16),
            pltpu.VMEM((2, 2, B, D), BF16),
            pltpu.SemaphoreType.DMA((NSEM,)),
            pltpu.SemaphoreType.DMA((NSEM,)),
            pltpu.SemaphoreType.DMA((rounds_r, 2)),
            pltpu.SemaphoreType.DMA((rounds_r, 2)),
            pltpu.SemaphoreType.DMA((rounds_c, 2)),
            pltpu.SemaphoreType.DMA((rounds_c, 2)),
        ],
        compiler_params=pltpu.CompilerParams(
            collective_id=0, has_side_effects=True, vmem_limit_bytes=67043328
        ),
    )(images, texts, audio)


def hand_over(a, b, c, x, y, z):
    x[...] = a[...]
    y[...] = b[...]
    z[...] = c[...]


def shards(images, texts, audio):
    outs = gradients(images, texts, audio)
    whole = pl.BlockSpec(memory_space=pltpu.VMEM)
    return pl.pallas_call(
        hand_over,
        out_shape=tuple(jax.ShapeDtypeStruct(o.shape, o.dtype) for o in outs),
        in_specs=[whole] * 3,
        out_specs=[whole] * 3,
    )(*outs)


def solution(mesh):
    by_row = P(("row", "col"), None)
    by_col = P(("col", "row"), None)
    return jax.shard_map(
        shards,
        mesh=mesh,
        in_specs=(by_row, by_col, by_col),
        out_specs=(by_row, by_col, by_col),
        check_vma=False,
    )
```

profile of v0, /device:TPU:0, one launch (start us, length us, event | category | flops | bytes accessed | tf_op | source)
XLA Modules:
  0.0 101.8 jit_solution(8223221291190443268)
XLA Ops:
  0.6 98.9 %shard_map.58 = (f32[128,768]{1,0:T(8,128)}, f32[128,768]{1,0:T(8,128)}, f32[128,768]{1,0:T(8,128)}) custom-call(bf16[128,768]{1,0:T(8,128)(2,1)} %img_hbm.1, bf16[128,768]{1,0:T(8,128)(2,1)} %txt_hbm.1, bf16[128,768]{1,0:T(8,128)(2,1)} %aud_hbm.1), custom_call_target="tpu_custom_call" | custom-call | tf_op jit(solution)/shard_map/pallas_call | solution.py:642
  99.5 2.3 %shard_map.59 = (f32[128,768]{1,0:T(8,128)}, f32[128,768]{1,0:T(8,128)}, f32[128,768]{1,0:T(8,128)}) custom-call(f32[128,768]{1,0:T(8,128)} %get-tuple-element.6.a, f32[128,768]{1,0:T(8,128)} %get-tuple-element.7.b, f32[128,768]{1,0:T(8,128)} %get-tuple-element.8.c), custom_call_target="tpu_custom_call" | custom-call | tf_op jit(solution)/shard_map/pallas_call | solution.py:710
where the time goes:
time: 102 us
  Pallas kernels  101 us (99%)
    pallas_call x1, Pallas kernels, gradients(): pl.pallas_call(kernel, out_shape=(shape, shape, shape), in_specs=[whole]...  98.9 us
    pallas_call x1, Pallas kernels, shards(): pl.pallas_call(hand_over, out_shape=tuple((jax.ShapeDtypeStruct(o.shape,...  2.27 us

commit v1 on v0

--- a/solution.py
+++ b/solution.py
@@ -132,15 +132,21 @@
         return at_zx(*place(h, first, second))
 
     def first_send(h):
-        for step in (1, 3):
-            net.send(("g1", h, step), image(0, 0, 64 * h, 64), image(*place(h, -step, 0), 64 * h, 64), half_dev(h, step, 0))
+        for turn in (0, 1):
+            for step in (1, 3):
+                at = 64 * h + 32 * (turn if step == 1 else 1 - turn)
+                net.send(("g1", h, step, turn), image(0, 0, at, 32), image(*place(h, -step, 0), at, 32), half_dev(h, step, 0))
+
+    def first_landed(h, step, turn):
+        at = 64 * h + 32 * (turn if step == 1 else 1 - turn)
+        net.wait(("g1", h, step, turn), image(*place(h, -step, 0), at, 32), half_dev(h, -step, 0))
 
     def second_send(h, f):
         for step in (1, 3):
             net.send(("g2", h, f, step), image(*place(h, f, 0), 64 * h, 64), image(*place(h, f, -step), 64 * h, 64), half_dev(h, 0, step))
 
     def first_forward(h, step):
-        net.wait(("g1", h, step), image(*place(h, -step, 0), 64 * h, 64), half_dev(h, -step, 0))
+        first_landed(h, step, 0)
         at = 64 * h + (0 if step == 1 else 32)
         net.send(("g1f", h, step), image(*place(h, -step, 0), at, 32), image(*place(h, 2, 0), at, 32), half_dev(h, step, 0))
 
@@ -160,16 +166,28 @@
             at = 64 * h + (0 if step == 1 else 32)
             net.wait(("g2f", h, f, step), image(*place(h, f, 2), at, 32), half_dev(h, 0, -step))
 
+    def col_at(step, turn):
+        return 64 * (turn if step == 1 else 1 - turn)
+
     def col_send(m):
-        for step in (1, 3):
-            net.send(("c1", m, step), column(m, 0, 1), column(m, -step, 1), at_y(step))
+        for turn in (0, 1):
+            for step in (1, 3):
+                at = col_at(step, turn)
+                net.send(("c1", m, step, turn), column(m, 0, 1, at, 64), column(m, -step, 1, at, 64), at_y(step))
         net.send(("cs", m, 0), column(m, 0, 1), column(m, 0, 0), at_y(0, 0))
+
+    def col_landed(m, step, turn):
+        net.wait(("c1", m, step, turn), column(m, -step, 1, col_at(step, turn), 64), at_y(-step))
 
     def col_forward(m):
         for step in (1, 3):
-            net.wait(("c1", m, step), column(m, -step, 1), at_y(-step))
-            at = 0 if step == 1 else 64
+            col_landed(m, step, 0)
+            at = col_at(step, 0)
             net.send(("c1f", m, step), column(m, -step, 1, at, 64), column(m, 2, 1, at, 64), at_y(step))
+
+    def col_side(m):
+        for step in (1, 3):
+            col_landed(m, step, 1)
             net.send(("cs", m, -step % 4), column(m, -step, 1), column(m, -step, 0), at_y(0, 0))
 
     def col_end(m):
@@ -196,25 +214,27 @@
 
     contract = (((1,), (1,)), ((), ()))
 
-    def similarity(m, lo, hi, left, right, first):
+    def similarity(m, lo, hi, left, right, first, base=0, rows=256):
         def body(i, carry):
-            at = pl.ds(pl.multiple_of(i * 256, 256), 256)
+            at = pl.ds(pl.multiple_of(base + i * rows, B), rows)
             cosine = lax.dot_general(
                 img[at, :], cols[m * 1024 + left : m * 1024 + right, :], contract, preferred_element_type=F32
             )
-            part = jnp.zeros((256, B), F32)
-            for j in range((right - left) // B):
-                piece = cosine[:, tile(j)]
-                kern = jnp.exp2(piece * (LOG2E / target_softness))
-                K[m, at, left + j * B : left + (j + 1) * B] = kern
-                soft = jnp.exp2(piece * (LOG2E / logit_softness))
-                E[at, m * 1024 + left + j * B : m * 1024 + left + (j + 1) * B] = soft.astype(BF16)
-                part = part + kern
-            for t in (0, 1):
-                total = row_part(part[t * B : (t + 1) * B])
+            for t in range(rows // B):
+                here = pl.ds(pl.multiple_of(base + i * rows + t * B, B), B)
+                part = jnp.zeros((B, B), F32)
+                for j in range((right - left) // B):
+                    piece = cosine[t * B : (t + 1) * B, tile(j)]
+                    kern = jnp.exp2(piece * (LOG2E / target_softness))
+                    K[m, here, left + j * B : left + (j + 1) * B] = kern
+                    soft = jnp.exp2(piece * (LOG2E / logit_softness))
+                    E[here, m * 1024 + left + j * B : m * 1024 + left + (j + 1) * B] = soft.astype(BF16)
+                    part = part + kern
+                total = row_part(part)
+                line = pl.ds(base // B + i * (rows // B) + t, 1)
                 if not first:
-                    total = total + rows_local[m, pl.ds(2 * i + t, 1), :]
-                rows_local[m, pl.ds(2 * i + t, 1), :] = total
+                    total = total + rows_local[m, line, :]
+                rows_local[m, line, :] = total
             return carry
 
         lax.fori_loop(lo, hi, body, 0)
@@ -228,8 +248,9 @@
     for step in (1, 3):
         for h in (0, 1):
             first_forward(h, step)
-    for f in (3, 1):
+    for f, step in ((3, 1), (1, 3)):
         for h in (0, 1):
+            first_landed(h, step, 1)
             second_send(h, f)
     col_forward(0)
     for h in (0, 1):
@@ -237,6 +258,7 @@
     for h in (0, 1):
         first_end(h)
         second_send(h, 2)
+    col_side(0)
     col_near(0)
     similarity(0, 6, 8, 256, 1024, True)
     for h in (0, 1):
@@ -244,6 +266,7 @@
     col_forward(1)
     for h in (0, 1):
         second_forward(h, 1)
+    col_side(1)
     col_near(1)
     similarity(1, 6, 8, 256, 1024, True)
     col_end(0)
@@ -258,12 +281,12 @@
         similarity(m, 3, 4, 256, 1024, True)
     for m in (0, 1):
         col_far(m)
-        similarity(m, 3, 8, 0, 256, False)
+        similarity(m, 0, 2, 0, 256, False, 768, 640)
     for f in (3, 1):
         for h in (0, 1):
             second_end(h, f)
     for m in (0, 1):
-        similarity(m, 1, 3, 0, 1024, True)
+        similarity(m, 0, 1, 0, 1024, True, 256, 512)
     for h in (0, 1):
         second_end(h, 2)
 
@@ -478,12 +501,9 @@
 
     def image_step(i, others):
         at = slice(i * 256, (i + 1) * 256)
-        for n in range(3):
-            out = slice(n * 256, (n + 1) * 256)
-            total = jnp.dot(S[at, :], cols[:, out], preferred_element_type=F32)
-            if n < len(others):
-                others[n]()
-            K[0, at, out] = total
+        for other in others:
+            other()
+        K[0, at, 0:D] = jnp.dot(S[at, :], cols[...], preferred_element_type=F32)
 
     def add_soft(i):
         for b in (2 * i, 2 * i + 1):
@@ -529,9 +549,8 @@
     down = (((0,), (0,)), ((), ()))
 
     def column_step(m, k):
-        total = lax.dot_general(
-            E[:, m * 1024 + k * 256 : m * 1024 + k * 256 + 256], img[...], down, preferred_element_type=F32
-        )
+        scored = E[:, m * 1024 + k * 256 : m * 1024 + k * 256 + 256]
+        total = lax.dot_general(scored, img[...], down, preferred_element_type=F32)
         gsib[m, k] = total[:B].astype(BF16)
         K[1, (m * 4 + k) * B : (m * 4 + k + 1) * B, 0:D] = total[B:]
         net.send(("sib", m, k), gsib.at[m, k], sibgot.at[m, k], at_y(0, 0))
@@ -549,60 +568,62 @@
     image_step(3, scores(7))
     for m in both:
         rows_back(rho, m, avec_turned[m] * rows_sum(ITERS, m) / rows_sum(ITERS + 1, m))
+    image_step(5, whole_scores(0, 1, 2))
+    add_soft(2)
     add_soft(0)
     reduce1(0, 2)
     reduce1(1, 2)
     reduce1(0, 1)
+    reduce1(1, 1)
+    reduce1(1, 3)
+    image_step(6, whole_scores(3, 4))
     add_soft(1)
     reduce1(0, 3)
+    image_step(4, whole_scores(5, 6, 7))
+    column_step(0, 0)
+    reduce2(0, 2, 0)
+    reduce2(0, 2, 1)
+    reduce2(1, 2, 0)
+    reduce2(1, 2, 1)
+    column_step(0, 2)
+    ring1(0)
     reduce1(0, 0)
-    add_soft(2)
-    reduce1(1, 1)
-    reduce1(1, 3)
+    column_step(1, 0)
+    add_soft(4)
+    reduce2(1, 1, 1)
+    reduce2(1, 3, 0)
+    reduce2(0, 1, 1)
+    column_step(0, 1)
+    ring1(1)
+    reduce2(0, 3, 0)
+    add_soft(5)
+    reduce2(0, 3, 1)
     add_soft(3)
     reduce1(1, 0)
-    image_step(4, whole_scores(0, 1, 2))
-    image_step(5, whole_scores(3, 4, 5))
-    whole_score(6)
-    whole_score(7)
-    column_step(0, 0)
-    add_soft(4)
-    add_soft(5)
-    for s in (0, 1):
-        reduce2(0, 2, s)
-        reduce2(1, 2, s)
-    column_step(1, 0)
-    ring1(0)
-    for s in (0, 1):
-        reduce2(0, 1, s)
-        reduce2(1, 1, s)
-    image_step(6, ())
-    ring1(1)
+    reduce2(0, 1, 0)
+    reduce3(0)
+    reduce2(1, 1, 0)
+    column_step(1, 2)
+    reduce3(1)
+    ring2(0, 0)
+    ring2(0, 1)
+    reduce2(1, 3, 1)
     add_soft(6)
-    for s in (0, 1):
-        reduce2(0, 3, s)
-        reduce2(1, 3, s)
-    image_step(7, ())
+    reduce2(0, 0, 1)
+    column_step(1, 3)
+    column_step(1, 1)
+    reduce2(1, 0, 0)
+    ring2(1, 1)
+    reduce2(0, 0, 0)
+    image_step(7, whole_scores())
     add_soft(7)
-    for s in (0, 1):
-        reduce2(0, 0, s)
-        reduce2(1, 0, s)
-    column_step(0, 1)
-    column_step(0, 2)
-    ring2(0, 0)
-    reduce3(0)
-    reduce3(1)
-    column_step(1, 1)
-    ring2(0, 1)
-    column_step(1, 2)
+    reduce4(0, 1)
+    reduce2(1, 0, 1)
     ring2(1, 0)
-    for h in (0, 1):
-        reduce4(h, 0)
+    reduce4(0, 0)
+    reduce4(1, 1)
+    reduce4(1, 0)
     column_step(0, 3)
-    ring2(1, 1)
-    for h in (0, 1):
-        reduce4(h, 1)
-    column_step(1, 3)
 
     def finish(raw_ref, out_ref, rows, g):
         values = raw_ref[rows, :].astype(F32)
@@ -617,11 +638,11 @@
         stores.append(pltpu.make_async_copy(src, dst, out_sem.at[len(stores)]))
         stores[-1].start()
 
+    finish(txt_in, out_txt, slice(0, B), ring3(0))
+    leave(out_txt, txt_out)
     for h in (0, 1):
         finish(img_in, out_img, slice(64 * h, 64 * h + 64), reduce5(h))
     leave(out_img, img_out)
-    finish(txt_in, out_txt, slice(0, B), ring3(0))
-    leave(out_txt, txt_out)
     finish(aud_in, out_aud, slice(0, B), ring3(1))
     leave(out_aud, aud_out)
 

time: 102 us -> 98.1 us (0.962)
  Pallas kernels: 101 us -> 97 us
    pallas_call x1, Pallas kernels: 98.9 us -> 94.8 us  [gradients(): pl.pallas_call(kernel, out_shape=(shape, shape, shape), in_specs=[whole]...]
where the time goes in v1:
time: 98.1 us; the launch traced here: 97.7 us
  Pallas kernels  97 us (99%)
    pallas_call x1, Pallas kernels, gradients(): pl.pallas_call(kernel, out_shape=(shape, shape, shape), in_specs=[whole]...  94.8 us
    pallas_call x1, Pallas kernels, shards(): pl.pallas_call(hand_over, out_shape=tuple((jax.ShapeDtypeStruct(o.shape,...  2.27 us

profile of v1, /device:TPU:0, one launch (start us, length us, event | category | flops | bytes accessed | tf_op | source)
XLA Modules:
  0.0 97.7 jit_solution(8922611784350175039)
XLA Ops:
  0.6 94.8 %shard_map.58 = (f32[128,768]{1,0:T(8,128)}, f32[128,768]{1,0:T(8,128)}, f32[128,768]{1,0:T(8,128)}) custom-call(bf16[128,768]{1,0:T(8,128)(2,1)} %img_hbm.1, bf16[128,768]{1,0:T(8,128)(2,1)} %txt_hbm.1, bf16[128,768]{1,0:T(8,128)(2,1)} %aud_hbm.1), custom_call_target="tpu_custom_call" | custom-call | tf_op jit(solution)/shard_map/pallas_call | solution.py:663
  95.4 2.3 %shard_map.59 = (f32[128,768]{1,0:T(8,128)}, f32[128,768]{1,0:T(8,128)}, f32[128,768]{1,0:T(8,128)}) custom-call(f32[128,768]{1,0:T(8,128)} %get-tuple-element.6.a, f32[128,768]{1,0:T(8,128)} %get-tuple-element.7.b, f32[128,768]{1,0:T(8,128)} %get-tuple-element.8.c), custom_call_target="tpu_custom_call" | custom-call | tf_op jit(solution)/shard_map/pallas_call | solution.py:731

commit v2 on v1

--- a/solution.py
+++ b/solution.py
@@ -407,7 +407,7 @@
         softmax(m)
         rows_send(ITERS + 1, m)
         cols_send(ITERS, m)
-    cuts = [0, 3, 6, 9, 12, 16]
+    cuts = [0, 2, 6, 9, 13, 16]
     for sweep in range(ITERS):
         for m in both:
             avec_turned[m] = 1.0 / rows_sum(sweep, m)

time: 98.1 us -> 98.1 us (level)
  no operation moved by 1% of the time
where the time goes in v2:
time: 98.1 us; the launch traced here: 97.7 us
  Pallas kernels  97 us (99%)
    pallas_call x1, Pallas kernels, gradients(): pl.pallas_call(kernel, out_shape=(shape, shape, shape), in_specs=[whole]...  94.8 us
    pallas_call x1, Pallas kernels, shards(): pl.pallas_call(hand_over, out_shape=tuple((jax.ShapeDtypeStruct(o.shape,...  2.27 us

profile of v2, /device:TPU:0, one launch (start us, length us, event | category | flops | bytes accessed | tf_op | source)
XLA Modules:
  0.0 97.7 jit_solution(3423050792651324130)
XLA Ops:
  0.6 94.8 %shard_map.58 = (f32[128,768]{1,0:T(8,128)}, f32[128,768]{1,0:T(8,128)}, f32[128,768]{1,0:T(8,128)}) custom-call(bf16[128,768]{1,0:T(8,128)(2,1)} %img_hbm.1, bf16[128,768]{1,0:T(8,128)(2,1)} %txt_hbm.1, bf16[128,768]{1,0:T(8,128)(2,1)} %aud_hbm.1), custom_call_target="tpu_custom_call" | custom-call | tf_op jit(solution)/shard_map/pallas_call | solution.py:663
  95.4 2.3 %shard_map.59 = (f32[128,768]{1,0:T(8,128)}, f32[128,768]{1,0:T(8,128)}, f32[128,768]{1,0:T(8,128)}) custom-call(f32[128,768]{1,0:T(8,128)} %get-tuple-element.6.a, f32[128,768]{1,0:T(8,128)} %get-tuple-element.7.b, f32[128,768]{1,0:T(8,128)} %get-tuple-element.8.c), custom_call_target="tpu_custom_call" | custom-call | tf_op jit(solution)/shard_map/pallas_call | solution.py:731
